TPU v7x, 32 devices: a whole 2x2x4 slice. The times are simulated.
32 devices in a mesh: dp: 16 (over z, y, core), mp: 2 (over x).
Axes of the slice: x: 2, y: 2, z: 4, core: 2. Of those that a mesh axis runs over, the one named last changes fastest.
Arguments:
- inputs: bfloat16 [65536, 1024], P(('dp', 'mp')), may hold values from -6 to 6
- rand_blocks: int32 [16, 16, 62, 3], P('dp', 'mp'), may hold values from 1 to 62
- ln1_gain: float32 [1024], replicated, may hold values from 0.1 to 1.9
- ln1_bias: float32 [1024], replicated, may hold values from -4 to 4
- w_qkv: bfloat16 [3, 1024, 1024], P(None, None, 'mp'), may hold values from -0.1875 to 0.1875
- w_out: bfloat16 [1024, 1024], P('mp'), may hold values from -1.5 to 1.5
- ln2_gain: float32 [1024], replicated, may hold values from 0.1 to 1.9
- ln2_bias: float32 [1024], replicated, may hold values from -4 to 4
- w_up: bfloat16 [1024, 4096], P(None, 'mp'), may hold values from -0.1875 to 0.1875
- b_up: float32 [4096], P('mp'), may hold values from -6 to 6
- w_down: bfloat16 [4096, 1024], P('mp'), may hold values from -0.09375 to 0.09375
- b_down: float32 [1024], replicated, may hold values from -6 to 6
- cotangent: bfloat16 [65536, 1024], P(('dp', 'mp')), may hold values from -6 to 6
Outputs:
- output: float32 [65536, 1024], P(('dp', 'mp'))
- input_grad: float32 [65536, 1024], P(('dp', 'mp'))
- d_ln1_gain: float32 [1024], replicated
- d_ln1_bias: float32 [1024], replicated
- d_w_qkv: float32 [3, 1024, 1024], P(None, None, 'mp')
- d_w_out: float32 [1024, 1024], P('mp')
- d_ln2_gain: float32 [1024], replicated
- d_ln2_bias: float32 [1024], replicated
- d_w_up: float32 [1024, 4096], P(None, 'mp')
- d_b_up: float32 [4096], P('mp')
- d_w_down: float32 [4096, 1024], P('mp')
- d_b_down: float32 [1024], replicated
Inputs may be any that keep to these rules, and one draw needn't show every extreme that they name: `rand_blocks`: a block may appear more than once in a list and may equal a window or global block.
All inputs are finite; a program needn't handle non-finite values.
Results may differ from a plain program's by a relative error of at most 0.02.
Values may be sent and summed in bfloat16 or wider, within the bound.
A program may use at most 320 MiB of HBM per device.

v0:
```python
from functools import partial
import jax
import jax.numpy as jnp
from jax import lax
from jax.sharding import PartitionSpec as P

BLOCK = 64
EPSILON = 1e-05
PLAIN = (((1,), (1,)), ((), ()))
ROWWISE = (((0,), (0,)), ((), ()))
HIGH = lax.Precision.HIGHEST


def norm_rows(values, scale_vec, offset):
    centered = values - jnp.mean(values, axis=-1, keepdims=True)
    inv_std = lax.rsqrt(jnp.mean(centered * centered, axis=-1, keepdims=True) + EPSILON)
    normed = centered * inv_std
    return (normed * scale_vec + offset, normed, inv_std)


def norm_back(normed, inv_std, scale_vec, gradient):
    scaled = gradient * scale_vec
    inner_term = (
        scaled
        - jnp.mean(scaled, axis=-1, keepdims=True)
        - normed * jnp.mean(scaled * normed, axis=-1, keepdims=True)
    )
    return (inv_std * inner_term, jnp.sum(gradient * normed, 0), jnp.sum(gradient, 0))


def gelu_tanh(values):
    return jax.nn.gelu(values, approximate=True)


def block_table(random_rows, num_blocks):
    rows_idx = jnp.arange(num_blocks, dtype=jnp.int32)[:, None]
    steps_off = jnp.arange(-1, 2, dtype=jnp.int32)[None, :]
    window = jnp.clip(rows_idx + steps_off, 0, num_blocks - 1)
    filler = jnp.zeros((1, random_rows.shape[1]), jnp.int32)
    chosen = jnp.concatenate([filler, random_rows, filler], 0)
    first_cols = jnp.zeros((num_blocks, 1), jnp.int32)
    last_cols = first_cols + (num_blocks - 1)
    return jnp.concatenate([first_cols, last_cols, window, chosen], 1)


def make_selector(table_grp, num_blocks):
    flat_table = table_grp.reshape(-1)
    return (flat_table[:, None] == jnp.arange(num_blocks, dtype=jnp.int32)[None, :]).astype(
        jnp.bfloat16
    )


def pick_blocks(selector, both_flat, per_query, block_rows, head_width):
    picked = jnp.dot(selector, both_flat, preferred_element_type=jnp.float32).astype(jnp.bfloat16)
    picked = picked.reshape(8, per_query, 2, block_rows, head_width)
    key_grp = picked[:, :, 0].reshape(8, per_query * block_rows, head_width)
    value_grp = picked[:, :, 1].reshape(8, per_query * block_rows, head_width)
    return (key_grp, value_grp)


def attend_item(operands):
    query, keys, values, table = operands
    num_blocks, per_query = table.shape
    seq_len, head_width = query.shape
    block_rows = seq_len // num_blocks
    scaling = head_width ** (-0.5)
    both_flat = jnp.stack(
        [
            keys.reshape(num_blocks, block_rows * head_width),
            values.reshape(num_blocks, block_rows * head_width),
        ],
        1,
    ).reshape(num_blocks, 2 * block_rows * head_width)
    query_groups = query.reshape(num_blocks // 8, 8, block_rows, head_width)
    table_groups = table.reshape(num_blocks // 8, 8, per_query)

    def group_scores(group_ops):
        query_grp, table_grp = group_ops
        selector = make_selector(table_grp, num_blocks)
        key_grp, value_grp = pick_blocks(selector, both_flat, per_query, block_rows, head_width)
        scores = (
            jnp.einsum("nqd,nkd->nqk", query_grp, key_grp, preferred_element_type=jnp.float32)
            * scaling
        )
        highest = jnp.max(scores, axis=-1, keepdims=True)
        shifted = jnp.exp(scores - highest)
        totals = jnp.sum(shifted, axis=-1, keepdims=True)
        weights_low = (shifted / totals).astype(jnp.bfloat16)
        mixed_grp = jnp.einsum(
            "nqk,nkd->nqd", weights_low, value_grp, preferred_element_type=jnp.float32
        )
        return (mixed_grp, (highest + jnp.log(totals))[..., 0])

    mixed, sparse_log = lax.map(group_scores, (query_groups, table_groups))
    mixed = mixed.reshape(seq_len, head_width)
    end_rows = jnp.concatenate([query[:block_rows], query[seq_len - block_rows :]], 0)
    glob_scores = (
        lax.dot_general(end_rows, keys, PLAIN, preferred_element_type=jnp.float32) * scaling
    )
    glob_high = jnp.max(glob_scores, axis=-1, keepdims=True)
    glob_exp = jnp.exp(glob_scores - glob_high)
    glob_total = jnp.sum(glob_exp, axis=-1, keepdims=True)
    glob_mixed = jnp.dot(
        (glob_exp / glob_total).astype(jnp.bfloat16), values, preferred_element_type=jnp.float32
    )
    mixed = mixed.at[:block_rows].set(glob_mixed[:block_rows])
    mixed = mixed.at[seq_len - block_rows :].set(glob_mixed[block_rows:])
    return (mixed.astype(jnp.bfloat16), sparse_log, (glob_high + jnp.log(glob_total))[:, 0])


def attend_back(operands):
    query, keys, values, table, out_grad, sparse_log, glob_log = operands
    num_blocks, per_query = table.shape
    seq_len, head_width = query.shape
    block_rows = seq_len // num_blocks
    scaling = head_width ** (-0.5)
    both_flat = jnp.stack(
        [
            keys.reshape(num_blocks, block_rows * head_width),
            values.reshape(num_blocks, block_rows * head_width),
        ],
        1,
    ).reshape(num_blocks, 2 * block_rows * head_width)
    query_groups = query.reshape(num_blocks // 8, 8, block_rows, head_width)
    table_groups = table.reshape(num_blocks // 8, 8, per_query)
    inner_blocks = jnp.arange(num_blocks) % (num_blocks - 1) != 0
    grad_blocks = out_grad.reshape(num_blocks, block_rows, head_width)
    grad_blocks = jnp.where(inner_blocks[:, None, None], grad_blocks, jnp.zeros_like(grad_blocks))
    grad_groups = grad_blocks.reshape(num_blocks // 8, 8, block_rows, head_width)

    def group_back(carry, group_ops):
        query_grp, table_grp, grad_grp, log_grp = group_ops
        selector = make_selector(table_grp, num_blocks)
        key_grp, value_grp = pick_blocks(selector, both_flat, per_query, block_rows, head_width)
        scores = (
            jnp.einsum("nqd,nkd->nqk", query_grp, key_grp, preferred_element_type=jnp.float32)
            * scaling
        )
        probs = jnp.exp(scores - log_grp[..., None])
        prob_grad = jnp.einsum(
            "nqd,nkd->nqk", grad_grp, value_grp, preferred_element_type=jnp.float32
        )
        inner_sum = jnp.sum(probs * prob_grad, axis=-1, keepdims=True)
        score_grad = (probs * (prob_grad - inner_sum)).astype(jnp.bfloat16)
        query_grad = (
            jnp.einsum("nqk,nkd->nqd", score_grad, key_grp, preferred_element_type=jnp.float32)
            * scaling
        )
        key_part = (
            jnp.einsum("nqk,nqd->nkd", score_grad, query_grp, preferred_element_type=jnp.float32)
            * scaling
        )
        value_part = jnp.einsum(
            "nqk,nqd->nkd", probs.astype(jnp.bfloat16), grad_grp, preferred_element_type=jnp.float32
        )
        parts = jnp.stack(
            [
                key_part.reshape(8 * per_query, block_rows * head_width),
                value_part.reshape(8 * per_query, block_rows * head_width),
            ],
            1,
        )
        parts = parts.reshape(8 * per_query, 2 * block_rows * head_width)
        carry = carry + lax.dot_general(
            selector.astype(jnp.float32),
            parts,
            ROWWISE,
            precision=HIGH,
            preferred_element_type=jnp.float32,
        )
        return (carry, query_grad)

    zero_blocks = jnp.zeros((num_blocks, 2 * block_rows * head_width), jnp.float32)
    accum, query_grad = lax.scan(
        group_back, zero_blocks, (query_groups, table_groups, grad_groups, sparse_log)
    )
    accum = accum.reshape(num_blocks, 2, block_rows, head_width)
    key_acc = accum[:, 0].reshape(seq_len, head_width)
    value_acc = accum[:, 1].reshape(seq_len, head_width)
    query_grad = query_grad.reshape(seq_len, head_width)
    end_rows = jnp.concatenate([query[:block_rows], query[seq_len - block_rows :]], 0)
    end_grad = jnp.concatenate([out_grad[:block_rows], out_grad[seq_len - block_rows :]], 0)
    glob_scores = (
        lax.dot_general(end_rows, keys, PLAIN, preferred_element_type=jnp.float32) * scaling
    )
    glob_probs = jnp.exp(glob_scores - glob_log[:, None])
    glob_pgrad = lax.dot_general(end_grad, values, PLAIN, preferred_element_type=jnp.float32)
    glob_inner = jnp.sum(glob_probs * glob_pgrad, axis=-1, keepdims=True)
    glob_sgrad = (glob_probs * (glob_pgrad - glob_inner)).astype(jnp.bfloat16)
    glob_qgrad = jnp.dot(glob_sgrad, keys, preferred_element_type=jnp.float32) * scaling
    query_grad = query_grad.at[:block_rows].add(glob_qgrad[:block_rows])
    query_grad = query_grad.at[seq_len - block_rows :].add(glob_qgrad[block_rows:])
    key_grad = (
        key_acc
        + lax.dot_general(glob_sgrad, end_rows, ROWWISE, preferred_element_type=jnp.float32)
        * scaling
    )
    value_grad = value_acc + lax.dot_general(
        glob_probs.astype(jnp.bfloat16), end_grad, ROWWISE, preferred_element_type=jnp.float32
    )
    return (query_grad, key_grad, value_grad)


def per_device(
    inputs,
    rand_blocks,
    ln1_gain,
    ln1_bias,
    w_qkv,
    w_out,
    ln2_gain,
    ln2_bias,
    w_up,
    b_up,
    w_down,
    b_down,
    cotangent,
):
    seqs_here = rand_blocks.shape[0]
    heads_here = rand_blocks.shape[1]
    item_count = seqs_here * heads_here
    head_width = w_qkv.shape[2] // heads_here
    residual_in = inputs.astype(jnp.float32)
    normed_one, normed_a, inv_a = norm_rows(residual_in, ln1_gain, ln1_bias)
    first_rows = lax.all_gather(normed_one.astype(jnp.bfloat16), "mp", axis=0, tiled=True)
    group_rows = first_rows.shape[0]
    seq_len = group_rows // seqs_here
    num_blocks = seq_len // BLOCK
    projected = jnp.einsum(
        "td,cde->cte", first_rows, w_qkv, preferred_element_type=jnp.float32
    ).astype(jnp.bfloat16)
    heads_qkv = projected.reshape(3, seqs_here, seq_len, heads_here, head_width).transpose(
        0, 1, 3, 2, 4
    )
    heads_qkv = heads_qkv.reshape(3, item_count, seq_len, head_width)
    tables = jax.vmap(partial(block_table, num_blocks=num_blocks))(
        rand_blocks.reshape(item_count, num_blocks - 2, rand_blocks.shape[3])
    )
    mixed, sparse_log, glob_log = lax.map(
        attend_item, (heads_qkv[0], heads_qkv[1], heads_qkv[2], tables)
    )
    attn_mix = (
        mixed.reshape(seqs_here, heads_here, seq_len, head_width)
        .transpose(0, 2, 1, 3)
        .reshape(group_rows, heads_here * head_width)
    )
    attn_out = lax.psum_scatter(
        jnp.dot(attn_mix, w_out, preferred_element_type=jnp.float32).astype(jnp.bfloat16),
        "mp",
        scatter_dimension=0,
        tiled=True,
    ).astype(jnp.float32)
    mid_resid = residual_in + attn_out
    normed_two, normed_b, inv_b = norm_rows(mid_resid, ln2_gain, ln2_bias)
    second_rows, grad_rows = (
        lax.all_gather(normed_two.astype(jnp.bfloat16), "mp", axis=0, tiled=True),
        lax.all_gather(cotangent, "mp", axis=0, tiled=True),
    )
    hidden_pre = jnp.dot(second_rows, w_up, preferred_element_type=jnp.float32) + b_up
    hidden_act = gelu_tanh(hidden_pre).astype(jnp.bfloat16)
    branch_out = lax.psum_scatter(
        jnp.dot(hidden_act, w_down, preferred_element_type=jnp.float32).astype(jnp.bfloat16),
        "mp",
        scatter_dimension=0,
        tiled=True,
    ).astype(jnp.float32)
    result = mid_resid + (branch_out + b_down)
    grad_own = cotangent.astype(jnp.float32)
    bias_down_grad = jnp.sum(grad_own, 0)
    down_grad = lax.dot_general(hidden_act, grad_rows, ROWWISE, preferred_element_type=jnp.float32)
    act_grad = lax.dot_general(grad_rows, w_down, PLAIN, preferred_element_type=jnp.float32)
    gelu_pull = jax.vjp(gelu_tanh, hidden_pre)[1]
    pre_grad = gelu_pull(act_grad)[0].astype(jnp.bfloat16)
    bias_up_grad = jnp.sum(pre_grad.astype(jnp.float32), 0)
    up_grad = lax.dot_general(second_rows, pre_grad, ROWWISE, preferred_element_type=jnp.float32)
    second_grad = lax.psum_scatter(
        lax.dot_general(pre_grad, w_up, PLAIN, preferred_element_type=jnp.float32).astype(
            jnp.bfloat16
        ),
        "mp",
        scatter_dimension=0,
        tiled=True,
    ).astype(jnp.float32)
    mid_part, gain_two_grad, bias_two_grad = norm_back(normed_b, inv_b, ln2_gain, second_grad)
    mid_grad = grad_own + mid_part
    attn_grad_rows = lax.all_gather(mid_grad.astype(jnp.bfloat16), "mp", axis=0, tiled=True)
    out_grad = lax.dot_general(
        attn_mix, attn_grad_rows, ROWWISE, preferred_element_type=jnp.float32
    )
    mix_grad = lax.dot_general(
        attn_grad_rows, w_out, PLAIN, preferred_element_type=jnp.float32
    ).astype(jnp.bfloat16)
    mix_items = (
        mix_grad.reshape(seqs_here, seq_len, heads_here, head_width)
        .transpose(0, 2, 1, 3)
        .reshape(item_count, seq_len, head_width)
    )
    query_grads, key_grads, value_grads = lax.map(
        attend_back,
        (heads_qkv[0], heads_qkv[1], heads_qkv[2], tables, mix_items, sparse_log, glob_log),
    )
    stacked = jnp.stack([query_grads, key_grads, value_grads]).astype(jnp.bfloat16)
    stacked = (
        stacked.reshape(3, seqs_here, heads_here, seq_len, head_width)
        .transpose(0, 1, 3, 2, 4)
        .reshape(3, group_rows, heads_here * head_width)
    )
    qkv_grad = jnp.einsum("td,cte->cde", first_rows, stacked, preferred_element_type=jnp.float32)
    first_grad = lax.psum_scatter(
        jnp.einsum("cte,cde->td", stacked, w_qkv, preferred_element_type=jnp.float32).astype(
            jnp.bfloat16
        ),
        "mp",
        scatter_dimension=0,
        tiled=True,
    ).astype(jnp.float32)
    input_part, gain_one_grad, bias_one_grad = norm_back(normed_a, inv_a, ln1_gain, first_grad)
    input_grad = mid_grad + input_part
    small_sums = lax.psum(
        (gain_one_grad, bias_one_grad, gain_two_grad, bias_two_grad, bias_down_grad), ("dp", "mp")
    )
    qkv_grad, out_grad, up_grad, bias_up_grad, down_grad = (
        lax.psum(qkv_grad.astype(jnp.bfloat16), "dp").astype(jnp.float32),
        lax.psum(out_grad.astype(jnp.bfloat16), "dp").astype(jnp.float32),
        lax.psum(up_grad.astype(jnp.bfloat16), "dp").astype(jnp.float32),
        lax.psum(bias_up_grad.astype(jnp.bfloat16), "dp").astype(jnp.float32),
        lax.psum(down_grad.astype(jnp.bfloat16), "dp").astype(jnp.float32),
    )
    return (
        result,
        input_grad,
        small_sums[0],
        small_sums[1],
        qkv_grad,
        out_grad,
        small_sums[2],
        small_sums[3],
        up_grad,
        bias_up_grad,
        down_grad,
        small_sums[4],
    )


def solution(mesh):
    return jax.shard_map(
        per_device,
        mesh=mesh,
        in_specs=(
            P(("dp", "mp"), None),
            P("dp", "mp", None, None),
            P(),
            P(),
            P(None, None, "mp"),
            P("mp", None),
            P(),
            P(),
            P(None, "mp"),
            P("mp"),
            P("mp", None),
            P(),
            P(("dp", "mp"), None),
        ),
        out_specs=(
            P(("dp", "mp"), None),
            P(("dp", "mp"), None),
            P(),
            P(),
            P(None, None, "mp"),
            P("mp", None),
            P(),
            P(),
            P(None, "mp"),
            P("mp"),
            P("mp", None),
            P(),
        ),
        check_vma=False,
    )
```

profile of v0, /device:TPU:0, one launch (start us, length us, event | category | flops | bytes accessed | tf_op | source)
XLA Modules:
  0.0 5234.4 jit_solution(17163692770296250939)
XLA Ops:
  17.8 106.0 %all-gather.5.cloned.1.call-done = bf16[4096,1024]{1,0:T(8,128)(2,1)} async-done(((bf16[2048,1024]{1,0:T(8,128)(2,1)}), bf16[4096,1024]{1,0:T(8,128)(2,1)}) %all-gather.5.cloned.1.call-update) | async-done | bytes 8388624 | tf_op jit(solution)/shard_map/all_gather | solution.py:225
  123.9 19.1 convolution_convert_fusion.2
  143.0 22.8 copy.97
  165.9 16.7 slice_bitcast_fusion
  182.6 964.2 %while.96 = (s32[]{:T(128)}, bf16[8,4096,64]{1,2,0:T(8,128)(2,1)}, f32[8,8,8,64]{3,2,1,0:T(8,128)}, f32[8,128]{1,0:T(8,128)}, bf16[8,4096,64]{2,1,0:T(8,128)(2,1...) while((s32[]{:T(128)}, bf16[8,4096,64]{1,2,0:T(8,128)(2,1)}, ...), condition=%wide.region_9.10_spmd, body=%wide.region_2.9_spmd.sunk | while | flops 275025280 | bytes 29968956 | solution.py:239
  200.6 93.5 %while.99 = (s32[]{:T(128)}, bf16[8,8,64,64]{3,2,1,0:T(8,128)(2,1)}, f32[8,8,64]{2,1,0:T(8,128)S(1)}, bf16[8,8,64,64]{3,2,1,0:T(8,128)(2,1)}, s32[8,8,8]{2,1,0:T...) while((s32[]{:T(128)}, bf16[8,8,64,64]{3,2,1,0:T(8,128)(2,1)}, f32[8,8,64]{2,1,0:T(8,128)S(1)}, ...), condition=%wide.region_6.6_spmd, body=%wide.region_3.5_spmd.sunk | while | flops 136580608 | bytes 10903893 | solution.py:94
  321.1 93.5 %while.99 = (s32[]{:T(128)}, bf16[8,8,64,64]{3,2,1,0:T(8,128)(2,1)}, f32[8,8,64]{2,1,0:T(8,128)S(1)}, bf16[8,8,64,64]{3,2,1,0:T(8,128)(2,1)}, s32[8,8,8]{2,1,0:T...) while((s32[]{:T(128)}, bf16[8,8,64,64]{3,2,1,0:T(8,128)(2,1)}, f32[8,8,64]{2,1,0:T(8,128)S(1)}, ...), condition=%wide.region_6.6_spmd, body=%wide.region_3.5_spmd.sunk | while | flops 136580608 | bytes 10903893 | solution.py:94
  441.6 93.5 %while.99 = (s32[]{:T(128)}, bf16[8,8,64,64]{3,2,1,0:T(8,128)(2,1)}, f32[8,8,64]{2,1,0:T(8,128)S(1)}, bf16[8,8,64,64]{3,2,1,0:T(8,128)(2,1)}, s32[8,8,8]{2,1,0:T...) while((s32[]{:T(128)}, bf16[8,8,64,64]{3,2,1,0:T(8,128)(2,1)}, f32[8,8,64]{2,1,0:T(8,128)S(1)}, ...), condition=%wide.region_6.6_spmd, body=%wide.region_3.5_spmd.sunk | while | flops 136580608 | bytes 10903893 | solution.py:94
  562.0 93.5 %while.99 = (s32[]{:T(128)}, bf16[8,8,64,64]{3,2,1,0:T(8,128)(2,1)}, f32[8,8,64]{2,1,0:T(8,128)S(1)}, bf16[8,8,64,64]{3,2,1,0:T(8,128)(2,1)}, s32[8,8,8]{2,1,0:T...) while((s32[]{:T(128)}, bf16[8,8,64,64]{3,2,1,0:T(8,128)(2,1)}, f32[8,8,64]{2,1,0:T(8,128)S(1)}, ...), condition=%wide.region_6.6_spmd, body=%wide.region_3.5_spmd.sunk | while | flops 136580608 | bytes 10903893 | solution.py:94
  682.5 93.5 %while.99 = (s32[]{:T(128)}, bf16[8,8,64,64]{3,2,1,0:T(8,128)(2,1)}, f32[8,8,64]{2,1,0:T(8,128)S(1)}, bf16[8,8,64,64]{3,2,1,0:T(8,128)(2,1)}, s32[8,8,8]{2,1,0:T...) while((s32[]{:T(128)}, bf16[8,8,64,64]{3,2,1,0:T(8,128)(2,1)}, f32[8,8,64]{2,1,0:T(8,128)S(1)}, ...), condition=%wide.region_6.6_spmd, body=%wide.region_3.5_spmd.sunk | while | flops 136580608 | bytes 10903893 | solution.py:94
  802.9 93.5 %while.99 = (s32[]{:T(128)}, bf16[8,8,64,64]{3,2,1,0:T(8,128)(2,1)}, f32[8,8,64]{2,1,0:T(8,128)S(1)}, bf16[8,8,64,64]{3,2,1,0:T(8,128)(2,1)}, s32[8,8,8]{2,1,0:T...) while((s32[]{:T(128)}, bf16[8,8,64,64]{3,2,1,0:T(8,128)(2,1)}, f32[8,8,64]{2,1,0:T(8,128)S(1)}, ...), condition=%wide.region_6.6_spmd, body=%wide.region_3.5_spmd.sunk | while | flops 136580608 | bytes 10903893 | solution.py:94
  923.4 93.5 %while.99 = (s32[]{:T(128)}, bf16[8,8,64,64]{3,2,1,0:T(8,128)(2,1)}, f32[8,8,64]{2,1,0:T(8,128)S(1)}, bf16[8,8,64,64]{3,2,1,0:T(8,128)(2,1)}, s32[8,8,8]{2,1,0:T...) while((s32[]{:T(128)}, bf16[8,8,64,64]{3,2,1,0:T(8,128)(2,1)}, f32[8,8,64]{2,1,0:T(8,128)S(1)}, ...), condition=%wide.region_6.6_spmd, body=%wide.region_3.5_spmd.sunk | while | flops 136580608 | bytes 10903893 | solution.py:94
  1043.8 93.5 %while.99 = (s32[]{:T(128)}, bf16[8,8,64,64]{3,2,1,0:T(8,128)(2,1)}, f32[8,8,64]{2,1,0:T(8,128)S(1)}, bf16[8,8,64,64]{3,2,1,0:T(8,128)(2,1)}, s32[8,8,8]{2,1,0:T...) while((s32[]{:T(128)}, bf16[8,8,64,64]{3,2,1,0:T(8,128)(2,1)}, f32[8,8,64]{2,1,0:T(8,128)S(1)}, ...), condition=%wide.region_6.6_spmd, body=%wide.region_3.5_spmd.sunk | while | flops 136580608 | bytes 10903893 | solution.py:94
  1146.8 10.5 convolution_convert_fusion.5
  1157.5 99.4 %reduce-scatter.5.cloned.1.call-done = bf16[2048,1024]{1,0:T(8,128)(2,1)} async-done(((bf16[4096,1024]{1,0:T(8,128)(2,1)}), bf16[2048,1024]{1,0:T(8,128)(2,1)}) %reduce-scatter.5.cloned.1.call-update) | async-done | bytes 4194320 | tf_op jit(solution)/shard_map/reduce_scatter | solution.py:247
  1269.3 103.5 %all-gather.7.cloned.1.call-done = bf16[4096,1024]{1,0:T(8,128)(2,1)} async-done(((bf16[2048,1024]{1,0:T(8,128)(2,1)}), bf16[4096,1024]{1,0:T(8,128)(2,1)}) %all-gather.7.cloned.1.call-update) | async-done | bytes 8388624 | tf_op jit(solution)/shard_map/all_gather | solution.py:256
  1372.8 34.0 multiply_convert_fusion.2
  1406.8 71.4 %all-gather.9.cloned.1.call-done = bf16[4096,1024]{1,0:T(8,128)(2,1)} async-done(((bf16[2048,1024]{1,0:T(8,128)(2,1)}), bf16[4096,1024]{1,0:T(8,128)(2,1)}) %all-gather.9.cloned.1.call-update) | async-done | bytes 8388624 | tf_op jit(solution)/shard_map/all_gather | solution.py:257
  1478.2 45.3 fusion.101
  1523.6 23.8 convolution_convert_fusion.3
  1547.4 99.4 %reduce-scatter.9.cloned.1.call-done = bf16[2048,1024]{1,0:T(8,128)(2,1)} async-done(((bf16[4096,1024]{1,0:T(8,128)(2,1)}), bf16[2048,1024]{1,0:T(8,128)(2,1)}) %reduce-scatter.9.cloned.1.call-update) | async-done | bytes 4194320 | tf_op jit(solution)/shard_map/reduce_scatter | solution.py:276
  1646.8 9.1 fusion.86
  1656.5 7.1 fusion.94
  1663.8 24.3 convolution_convert_fusion.8
  1688.1 23.7 convolution_convert_fusion.7
  1711.8 56.0 %all-gather.11.cloned.1.call-done = bf16[4096,1024]{1,0:T(8,128)(2,1)} async-done(((bf16[2048,1024]{1,0:T(8,128)(2,1)}), bf16[4096,1024]{1,0:T(8,128)(2,1)}) %all-gather.11.cloned.1.call-update) | async-done | bytes 8388624 | tf_op jit(solution)/shard_map/all_gather | solution.py:286
  1767.9 10.1 convolution_convert_fusion.6
  1778.0 8.3 copy.100
  1786.3 2913.1 %while.98 = (s32[]{:T(128)}, bf16[8,4096,64]{1,2,0:T(8,128)(2,1)}, bf16[8,4096,64]{1,2,0:T(8,128)(2,1)}, bf16[8,4096,64]{1,2,0:T(8,128)(2,1)}, bf16[8,4096,64]{2...) while((s32[]{:T(128)}, bf16[8,4096,64]{1,2,0:T(8,128)(2,1)}, ...), condition=%wide.region_22.23_spmd, body=%wide.region_17.22_spmd.sunk | while | flops 983490496 | bytes 111270584 | solution.py:298
  1809.6 307.4 %while.100 = (s32[]{:T(128)}, f32[64,8192]{1,0:T(8,128)}, f32[8,8,64,64]{3,2,1,0:T(8,128)}, s32[8,8,8]{2,1,0:T(8,128)S(1)}, bf16[8,8,64,64]{3,2,1,0:T(8,128)(2,1...) while((s32[]{:T(128)}, f32[64,8192]{1,0:T(8,128)}, ...), condition=%wide.region_20.20_spmd.clone, body=%wide.region_18.19_spmd.clone.sunk | while | flops 642031104 | bytes 48511176 | solution.py:174
  2173.7 307.4 %while.100 = (s32[]{:T(128)}, f32[64,8192]{1,0:T(8,128)}, f32[8,8,64,64]{3,2,1,0:T(8,128)}, s32[8,8,8]{2,1,0:T(8,128)S(1)}, bf16[8,8,64,64]{3,2,1,0:T(8,128)(2,1...) while((s32[]{:T(128)}, f32[64,8192]{1,0:T(8,128)}, ...), condition=%wide.region_20.20_spmd.clone, body=%wide.region_18.19_spmd.clone.sunk | while | flops 642031104 | bytes 48511176 | solution.py:174
  2537.7 307.4 %while.100 = (s32[]{:T(128)}, f32[64,8192]{1,0:T(8,128)}, f32[8,8,64,64]{3,2,1,0:T(8,128)}, s32[8,8,8]{2,1,0:T(8,128)S(1)}, bf16[8,8,64,64]{3,2,1,0:T(8,128)(2,1...) while((s32[]{:T(128)}, f32[64,8192]{1,0:T(8,128)}, ...), condition=%wide.region_20.20_spmd.clone, body=%wide.region_18.19_spmd.clone.sunk | while | flops 642031104 | bytes 48511176 | solution.py:174
  2901.8 307.4 %while.100 = (s32[]{:T(128)}, f32[64,8192]{1,0:T(8,128)}, f32[8,8,64,64]{3,2,1,0:T(8,128)}, s32[8,8,8]{2,1,0:T(8,128)S(1)}, bf16[8,8,64,64]{3,2,1,0:T(8,128)(2,1...) while((s32[]{:T(128)}, f32[64,8192]{1,0:T(8,128)}, ...), condition=%wide.region_20.20_spmd.clone, body=%wide.region_18.19_spmd.clone.sunk | while | flops 642031104 | bytes 48511176 | solution.py:174
  3265.9 307.4 %while.100 = (s32[]{:T(128)}, f32[64,8192]{1,0:T(8,128)}, f32[8,8,64,64]{3,2,1,0:T(8,128)}, s32[8,8,8]{2,1,0:T(8,128)S(1)}, bf16[8,8,64,64]{3,2,1,0:T(8,128)(2,1...) while((s32[]{:T(128)}, f32[64,8192]{1,0:T(8,128)}, ...), condition=%wide.region_20.20_spmd.clone, body=%wide.region_18.19_spmd.clone.sunk | while | flops 642031104 | bytes 48511176 | solution.py:174
  3629.9 307.4 %while.100 = (s32[]{:T(128)}, f32[64,8192]{1,0:T(8,128)}, f32[8,8,64,64]{3,2,1,0:T(8,128)}, s32[8,8,8]{2,1,0:T(8,128)S(1)}, bf16[8,8,64,64]{3,2,1,0:T(8,128)(2,1...) while((s32[]{:T(128)}, f32[64,8192]{1,0:T(8,128)}, ...), condition=%wide.region_20.20_spmd.clone, body=%wide.region_18.19_spmd.clone.sunk | while | flops 642031104 | bytes 48511176 | solution.py:174
  3994.0 307.4 %while.100 = (s32[]{:T(128)}, f32[64,8192]{1,0:T(8,128)}, f32[8,8,64,64]{3,2,1,0:T(8,128)}, s32[8,8,8]{2,1,0:T(8,128)S(1)}, bf16[8,8,64,64]{3,2,1,0:T(8,128)(2,1...) while((s32[]{:T(128)}, f32[64,8192]{1,0:T(8,128)}, ...), condition=%wide.region_20.20_spmd.clone, body=%wide.region_18.19_spmd.clone.sunk | while | flops 642031104 | bytes 48511176 | solution.py:174
  4358.0 307.4 %while.100 = (s32[]{:T(128)}, f32[64,8192]{1,0:T(8,128)}, f32[8,8,64,64]{3,2,1,0:T(8,128)}, s32[8,8,8]{2,1,0:T(8,128)S(1)}, bf16[8,8,64,64]{3,2,1,0:T(8,128)(2,1...) while((s32[]{:T(128)}, f32[64,8192]{1,0:T(8,128)}, ...), condition=%wide.region_20.20_spmd.clone, body=%wide.region_18.19_spmd.clone.sunk | while | flops 642031104 | bytes 48511176 | solution.py:174
  4699.4 8.0 pad_maximum_fusion.6
  4707.5 11.5 convolution_convert_fusion.9
  4719.0 14.5 convert_bitcast_fusion.3
  4733.6 18.4 bitcast_convert_fusion
  4752.0 23.6 convolution_convert_fusion.4
  4776.3 34.9 psum.77
  4811.8 154.5 %all-reduce.4.cloned.1.call-done = (bf16[3,1024,512]{1,2,0:T(8,128)(2,1)}, bf16[512,1024]{1,0:T(8,128)(2,1)}, bf16[1024,2048]{1,0:T(8,128)(2,1)}, bf16[2048,1024]{1,0:T(8,128)(2,1)}) async-done(((bf16[3,1024,512]{1,2,0:T(8,128)(2,1)}, bf16[512,1024]{1,0:T(8,128)(2,1)}, bf16[1024,2048]{1,0:T(8,128)(2,1)}, bf16[2048,1024]{1,0:T(8,128)(2,1)}), (bf16[3,1024,512]{1,2,0:T(8,128)(2,1)}, ...) | async-done | bytes 12582928 | tf_op jit(solution)/shard_map/psum | solution.py:323
  4985.9 82.6 %reduce-scatter.11.cloned.1.call-done = bf16[2048,1024]{1,0:T(8,128)(2,1)} async-done(((bf16[4096,1024]{1,0:T(8,128)(2,1)}), bf16[2048,1024]{1,0:T(8,128)(2,1)}) %reduce-scatter.11.cloned.1.call-update) | async-done | bytes 4194320 | tf_op jit(solution)/shard_map/reduce_scatter | solution.py:309
  5074.7 96.1 %reduce-scatter.7.cloned.1.call-done = bf16[2048,1024]{1,0:T(8,128)(2,1)} async-done(((bf16[4096,1024]{1,0:T(8,128)(2,1)}), bf16[2048,1024]{1,0:T(8,128)(2,1)}) %reduce-scatter.7.cloned.1.call-update) | async-done | bytes 4194320 | tf_op jit(solution)/shard_map/reduce_scatter | solution.py:261
  5170.8 17.0 fusion.80
  5187.8 39.9 all-reduce
  (2701 shorter events, 3920.6 us)
Async XLA Ops:
  7.2 116.7 %copy-start = (bf16[3,1024,512]{2,1,0:T(8,128)(2,1)S(1)}, bf16[3,1024,512]{2,1,0:T(8,128)(2,1)}, u32[]{:S(2)}) copy-start(bf16[3,1024,512]{2,1,0:T(8,128)(2,1)} %param.33) | copy-start | bytes 9437188
  7.2 6.8 copy-start.33
  7.2 6.8 copy-start.38
  7.2 116.6 %all-gather.5.cloned.1.call-start = ((), (), s32[]{:S(2)}) async-start(), calls=%async_computation.4 | async-start | bytes 12582912 | tf_op jit(solution)/shard_map/all_gather | solution.py:225
  7.3 6.7 copy-start.5
  10.3 7.1 copy-start.37
  17.0 1239.9 %reduce-scatter.5.cloned.1.call-start = ((), (), s32[]{:S(2)}) async-start(), calls=%async_computation.5 | async-start | bytes 12582912 | tf_op jit(solution)/shard_map/reduce_scatter | solution.py:247
  1146.8 10.6 copy-start.15
  1157.4 107.8 %copy-start.30 = (f32[1024]{0:T(1024)S(1)}, f32[1024]{0:T(1024)}, u32[]{:S(2)}) copy-start(f32[1024]{0:T(1024)} %param.35) | copy-start | bytes 12292
  1157.4 107.8 %copy-start.39 = (f32[1024]{0:T(1024)S(1)}, f32[1024]{0:T(1024)}, u32[]{:S(2)}) copy-start(f32[1024]{0:T(1024)} %param.36) | copy-start | bytes 12292
  1157.4 215.4 %all-gather.7.cloned.1.call-start = ((), (), s32[]{:S(2)}) async-start(), calls=%async_computation.6 | async-start | bytes 12582912 | tf_op jit(solution)/shard_map/all_gather | solution.py:256
  1256.9 4.8 copy-start.6
  1256.9 5.9 copy-start.10
  1265.2 107.6 %copy-start.43 = (f32[2048]{0:T(1024)S(1)}, f32[2048]{0:T(1024)}, u32[]{:S(2)}) copy-start(f32[2048]{0:T(1024)} %param.38) | copy-start | bytes 24580
  1268.7 209.6 %all-gather.9.cloned.1.call-start = ((), (), s32[]{:S(2)}) async-start(), calls=%async_computation.8 | async-start | bytes 12582912 | tf_op jit(solution)/shard_map/all_gather | solution.py:257
  1269.3 377.5 %reduce-scatter.9.cloned.1.call-start = ((), (), s32[]{:S(2)}) async-start(), calls=%async_computation.9 | async-start | bytes 12582912 | tf_op jit(solution)/shard_map/reduce_scatter | solution.py:276
  1547.3 99.5 %copy-start.17 = (f32[2048]{0:T(1024)S(1)}, f32[2048]{0:T(1024)}, u32[]{:S(2)}) copy-start(f32[2048]{0:T(1024)} %copy-done.16) | copy-start | bytes 24580
  1547.3 99.5 %copy-start.22 = (f32[2048]{0:T(1024)S(1)}, f32[2048]{0:T(1024)}, u32[]{:S(2)}) copy-start(f32[2048]{0:T(1024)} %copy-done.21) | copy-start | bytes 24580
  1547.3 99.5 %copy-start.31 = (f32[1024]{0:T(1024)S(1)}, f32[1024]{0:T(1024)}, u32[]{:S(2)}) copy-start(f32[1024]{0:T(1024)} %param.35) | copy-start | bytes 12292
  1547.3 220.5 %all-gather.11.cloned.1.call-start = ((), (), s32[]{:S(2)}) async-start(), calls=%async_computation.10 | async-start | bytes 12582912 | tf_op jit(solution)/shard_map/all_gather | solution.py:286
  1646.8 9.7 copy-start.7
  1646.8 9.7 copy-start.11
  1646.8 9.7 copy-start.12
  1663.7 3302.6 %all-reduce.4.cloned.1.call-start = ((), (), s32[]{:S(2)}) async-start(), calls=%async_computation.12 | async-start | bytes 25165824 | tf_op jit(solution)/shard_map/psum | solution.py:323
  1818.4 3.3 copy-start.2
  1933.3 3.3 copy-start.2
  2182.4 3.3 copy-start.2
  2451.3 3.3 copy-start.2
  2815.4 3.3 copy-start.2
  3274.6 3.3 copy-start.2
  4699.4 8.0 copy-start.42
  4699.4 19.5 slice-start
  4707.4 11.5 copy-start.13
  4707.5 11.5 slice-start.1
  4733.5 335.0 %reduce-scatter.11.cloned.1.call-start = ((), (), s32[]{:S(2)}) async-start(), calls=%async_computation.11 | async-start | bytes 12582912 | tf_op jit(solution)/shard_map/reduce_scatter | solution.py:309
  4752.0 418.8 %reduce-scatter.7.cloned.1.call-start = ((), (), s32[]{:S(2)}) async-start(), calls=%async_computation.7 | async-start | bytes 12582912 | tf_op jit(solution)/shard_map/reduce_scatter | solution.py:261
  4966.3 6.8 copy-start.14
  4977.6 91.0 %copy-start.20 = (f32[2048]{0:T(1024)S(1)}, f32[2048]{0:T(1024)}, u32[]{:S(2)}) copy-start(f32[2048]{0:T(1024)} %copy-done.19) | copy-start | bytes 24580
  4977.6 91.0 %copy-start.25 = (f32[2048]{0:T(1024)S(1)}, f32[2048]{0:T(1024)}, u32[]{:S(2)}) copy-start(f32[2048]{0:T(1024)} %copy-done.24) | copy-start | bytes 24580
  4977.6 91.0 %copy-start.34 = (f32[1024]{0:T(1024)S(1)}, f32[1024]{0:T(1024)}, u32[]{:S(2)}) copy-start(f32[1024]{0:T(1024)} %param.31) | copy-start | bytes 12292
  4977.6 193.2 %copy-start.18 = (f32[2048]{0:T(1024)S(1)}, f32[2048]{0:T(1024)}, u32[]{:S(2)}) copy-start(f32[2048]{0:T(1024)} %copy-done.16) | copy-start | bytes 24580
  4977.6 193.2 %copy-start.23 = (f32[2048]{0:T(1024)S(1)}, f32[2048]{0:T(1024)}, u32[]{:S(2)}) copy-start(f32[2048]{0:T(1024)} %copy-done.21) | copy-start | bytes 24580
  4977.6 193.2 %copy-start.27 = (f32[2048]{0:T(1024)S(1)}, f32[2048]{0:T(1024)}, u32[]{:S(2)}) copy-start(f32[2048]{0:T(1024)} %copy-done.26) | copy-start | bytes 24580
  4977.6 193.2 %copy-start.29 = (f32[2048]{0:T(1024)S(1)}, f32[2048]{0:T(1024)}, u32[]{:S(2)}) copy-start(f32[2048]{0:T(1024)} %copy-done.28) | copy-start | bytes 24580
  4977.6 193.2 %copy-start.32 = (f32[1024]{0:T(1024)S(1)}, f32[1024]{0:T(1024)}, u32[]{:S(2)}) copy-start(f32[1024]{0:T(1024)} %param.35) | copy-start | bytes 12292
  4977.6 193.2 %copy-start.40 = (f32[1024]{0:T(1024)S(1)}, f32[1024]{0:T(1024)}, u32[]{:S(2)}) copy-start(f32[1024]{0:T(1024)} %param.40) | copy-start | bytes 12292
  5074.7 113.1 %copy-start.35 = (f32[1024]{0:T(1024)S(1)}, f32[1024]{0:T(1024)}, u32[]{:S(2)}) copy-start(f32[1024]{0:T(1024)} %get-tuple-element.546) | copy-start | bytes 12292
  5074.7 113.1 %copy-start.36 = (f32[1024]{0:T(1024)S(1)}, f32[1024]{0:T(1024)}, u32[]{:S(2)}) copy-start(f32[1024]{0:T(1024)} %get-tuple-element.552) | copy-start | bytes 12292
  (217 other events, 337.3 us)
Sparse Core Ops, SparseCore 0:
  17.1 106.6 all-gather.4
  1157.5 99.3 reduce-scatter.4
  1268.8 103.9 all-gather.6
  1374.2 103.9 all-gather.8
  1547.5 99.2 reduce-scatter.8
  1663.8 103.9 all-gather.10
  4733.6 232.6 all-reduce.3
  4969.1 99.3 reduce-scatter.10
  5071.4 99.3 reduce-scatter.6
where the time goes:
time: 5280 us; the launch traced here: 5230 us
  local copies, waits for them, and re-layouts  2110 us (40%)
  matrix products  1870 us (35%)
  waiting for transfers between devices  870 us (16%)
  other arithmetic  290 us (5%)
  blocking collectives  74.8 us (1%)
    reshape x128, local copies, waits for them, and re-layouts, pick_blocks(): picked = picked.reshape(8, per_query, 2, block_rows, head_width)  543 us
    reshape x128, local copies, waits for them, and re-layouts, group_back(): jnp.stack([key_part.reshape(8 * per_query, block_rows * head_width), valu...  373 us
    dot_general x128, matrix products, pick_blocks(): jnp.dot(selector, both_flat, preferred_element_type=jnp.float32)  344 us
    dot_general x64, matrix products, group_back(): lax.dot_general(selector.astype(jnp.float32), parts, ROWWISE, precision=H...  303 us
    mul x64, local copies, waits for them, and re-layouts, group_back(): jnp.einsum('nqk,nqd->nkd', score_grad, query_grp, preferred_element_type=...  207 us
    dot_general x64, matrix products, group_back(): jnp.einsum('nqk,nqd->nkd', probs.astype(jnp.bfloat16), grad_grp, preferre...  200 us
    psum x1, waiting for transfers between devices, per_device(): lax.psum(qkv_grad.astype(jnp.bfloat16), 'dp').astype(jnp.float32)  154 us
    dot_general x64, matrix products, group_back(): jnp.einsum('nqk,nkd->nqd', score_grad, key_grp, preferred_element_type=jn...  154 us
  transfers between devices with their start and end apart: 9, of which 9 were waited for; matrix products, arithmetic and copies ran while one was open for 3% of the time, Pallas kernels for 0%

commit v1 on v0

--- a/solution.py
+++ b/solution.py
@@ -319,8 +319,9 @@
     small_sums = lax.psum(
         (gain_one_grad, bias_one_grad, gain_two_grad, bias_two_grad, bias_down_grad), ("dp", "mp")
     )
+    chains_obtain = lambda piece_in, peer_axis: jnp.sum(lax.all_gather(piece_in, peer_axis), axis=0)
     qkv_grad, out_grad, up_grad, bias_up_grad, down_grad = (
-        lax.psum(qkv_grad.astype(jnp.bfloat16), "dp").astype(jnp.float32),
+        chains_obtain(qkv_grad.astype(jnp.bfloat16), "dp").astype(jnp.float32),
         lax.psum(out_grad.astype(jnp.bfloat16), "dp").astype(jnp.float32),
         lax.psum(up_grad.astype(jnp.bfloat16), "dp").astype(jnp.float32),
         lax.psum(bias_up_grad.astype(jnp.bfloat16), "dp").astype(jnp.float32),

time: 5280 us -> 5260 us (level)
    all_gather x0 -> x1, waiting for transfers between devices: none -> 189 us  [per_device(): lax.all_gather(piece_in, peer_axis)]
    psum x1, waiting for transfers between devices: 154 us -> 0.01 us  [per_device(): lax.psum(out_grad.astype(jnp.bfloat16), 'dp').astype(jnp.float32)]
    reduce_scatter x1, waiting for transfers between devices: 82.6 us -> 5.12 us  [per_device(): lax.psum_scatter(jnp.einsum('cte,cde->td', stacked, w_qkv, preferred_elem...]
  transfers between devices with their start and end apart: 9 -> 10, of which waited for: 9 -> 9; matrix products, arithmetic and copies ran while one was open for 3% -> 57% of each run, Pallas kernels for 0% -> 0%
where the time goes in v1:
time: 5260 us; the launch traced here: 5210 us
  local copies, waits for them, and re-layouts  2120 us (40%)
  matrix products  1870 us (36%)
  waiting for transfers between devices  826 us (16%)
  other arithmetic  307 us (6%)
  blocking collectives  75.6 us (1%)
    reshape x128, local copies, waits for them, and re-layouts, pick_blocks(): picked = picked.reshape(8, per_query, 2, block_rows, head_width)  543 us
    reshape x128, local copies, waits for them, and re-layouts, group_back(): jnp.stack([key_part.reshape(8 * per_query, block_rows * head_width), valu...  372 us
    dot_general x128, matrix products, pick_blocks(): jnp.dot(selector, both_flat, preferred_element_type=jnp.float32)  341 us
    dot_general x64, matrix products, group_back(): lax.dot_general(selector.astype(jnp.float32), parts, ROWWISE, precision=H...  303 us
    mul x64, local copies, waits for them, and re-layouts, group_back(): jnp.einsum('nqk,nqd->nkd', score_grad, query_grp, preferred_element_type=...  206 us
    dot_general x64, matrix products, group_back(): jnp.einsum('nqk,nqd->nkd', probs.astype(jnp.bfloat16), grad_grp, preferre...  200 us
    all_gather x1, waiting for transfers between devices, per_device(): lax.all_gather(piece_in, peer_axis)  189 us
    dot_general x64, matrix products, group_back(): jnp.einsum('nqk,nkd->nqd', score_grad, key_grp, preferred_element_type=jn...  155 us
  transfers between devices with their start and end apart: 10, of which 9 were waited for; matrix products, arithmetic and copies ran while one was open for 57% of the time, Pallas kernels for 0%

profile of v1, /device:TPU:0, one launch (start us, length us, event | category | flops | bytes accessed | tf_op | source)
XLA Modules:
  0.0 5214.7 jit_solution(4548712589432820216)
XLA Ops:
  17.9 106.0 %all-gather.7.cloned.1.call-done = bf16[4096,1024]{1,0:T(8,128)(2,1)} async-done(((bf16[2048,1024]{1,0:T(8,128)(2,1)}), bf16[4096,1024]{1,0:T(8,128)(2,1)}) %all-gather.7.cloned.1.call-update) | async-done | bytes 8388624 | tf_op jit(solution)/shard_map/all_gather | solution.py:225
  123.9 19.1 convolution_convert_fusion.2
  143.0 22.8 copy.94
  165.8 16.7 slice_bitcast_fusion
  182.5 961.9 %while.96 = (s32[]{:T(128)}, bf16[8,4096,64]{1,2,0:T(8,128)(2,1)}, f32[8,8,8,64]{3,2,1,0:T(8,128)}, f32[8,128]{1,0:T(8,128)}, bf16[8,4096,64]{2,1,0:T(8,128)(2,1...) while((s32[]{:T(128)}, bf16[8,4096,64]{1,2,0:T(8,128)(2,1)}, ...), condition=%wide.region_9.10_spmd, body=%wide.region_2.9_spmd.sunk | while | flops 275025280 | bytes 29968956 | solution.py:239
  200.6 93.2 %while.99 = (s32[]{:T(128)}, bf16[8,8,64,64]{3,2,1,0:T(8,128)(2,1)}, f32[8,8,64]{2,1,0:T(8,128)S(1)}, bf16[8,8,64,64]{3,2,1,0:T(8,128)(2,1)}, s32[8,8,8]{2,1,0:T...) while((s32[]{:T(128)}, bf16[8,8,64,64]{3,2,1,0:T(8,128)(2,1)}, f32[8,8,64]{2,1,0:T(8,128)S(1)}, ...), condition=%wide.region_6.6_spmd, body=%wide.region_3.5_spmd.sunk | while | flops 136580608 | bytes 10903893 | solution.py:94
  320.7 93.2 %while.99 = (s32[]{:T(128)}, bf16[8,8,64,64]{3,2,1,0:T(8,128)(2,1)}, f32[8,8,64]{2,1,0:T(8,128)S(1)}, bf16[8,8,64,64]{3,2,1,0:T(8,128)(2,1)}, s32[8,8,8]{2,1,0:T...) while((s32[]{:T(128)}, bf16[8,8,64,64]{3,2,1,0:T(8,128)(2,1)}, f32[8,8,64]{2,1,0:T(8,128)S(1)}, ...), condition=%wide.region_6.6_spmd, body=%wide.region_3.5_spmd.sunk | while | flops 136580608 | bytes 10903893 | solution.py:94
  441.0 93.2 %while.99 = (s32[]{:T(128)}, bf16[8,8,64,64]{3,2,1,0:T(8,128)(2,1)}, f32[8,8,64]{2,1,0:T(8,128)S(1)}, bf16[8,8,64,64]{3,2,1,0:T(8,128)(2,1)}, s32[8,8,8]{2,1,0:T...) while((s32[]{:T(128)}, bf16[8,8,64,64]{3,2,1,0:T(8,128)(2,1)}, f32[8,8,64]{2,1,0:T(8,128)S(1)}, ...), condition=%wide.region_6.6_spmd, body=%wide.region_3.5_spmd.sunk | while | flops 136580608 | bytes 10903893 | solution.py:94
  561.2 93.2 %while.99 = (s32[]{:T(128)}, bf16[8,8,64,64]{3,2,1,0:T(8,128)(2,1)}, f32[8,8,64]{2,1,0:T(8,128)S(1)}, bf16[8,8,64,64]{3,2,1,0:T(8,128)(2,1)}, s32[8,8,8]{2,1,0:T...) while((s32[]{:T(128)}, bf16[8,8,64,64]{3,2,1,0:T(8,128)(2,1)}, f32[8,8,64]{2,1,0:T(8,128)S(1)}, ...), condition=%wide.region_6.6_spmd, body=%wide.region_3.5_spmd.sunk | while | flops 136580608 | bytes 10903893 | solution.py:94
  681.3 93.2 %while.99 = (s32[]{:T(128)}, bf16[8,8,64,64]{3,2,1,0:T(8,128)(2,1)}, f32[8,8,64]{2,1,0:T(8,128)S(1)}, bf16[8,8,64,64]{3,2,1,0:T(8,128)(2,1)}, s32[8,8,8]{2,1,0:T...) while((s32[]{:T(128)}, bf16[8,8,64,64]{3,2,1,0:T(8,128)(2,1)}, f32[8,8,64]{2,1,0:T(8,128)S(1)}, ...), condition=%wide.region_6.6_spmd, body=%wide.region_3.5_spmd.sunk | while | flops 136580608 | bytes 10903893 | solution.py:94
  801.5 93.2 %while.99 = (s32[]{:T(128)}, bf16[8,8,64,64]{3,2,1,0:T(8,128)(2,1)}, f32[8,8,64]{2,1,0:T(8,128)S(1)}, bf16[8,8,64,64]{3,2,1,0:T(8,128)(2,1)}, s32[8,8,8]{2,1,0:T...) while((s32[]{:T(128)}, bf16[8,8,64,64]{3,2,1,0:T(8,128)(2,1)}, f32[8,8,64]{2,1,0:T(8,128)S(1)}, ...), condition=%wide.region_6.6_spmd, body=%wide.region_3.5_spmd.sunk | while | flops 136580608 | bytes 10903893 | solution.py:94
  921.7 93.2 %while.99 = (s32[]{:T(128)}, bf16[8,8,64,64]{3,2,1,0:T(8,128)(2,1)}, f32[8,8,64]{2,1,0:T(8,128)S(1)}, bf16[8,8,64,64]{3,2,1,0:T(8,128)(2,1)}, s32[8,8,8]{2,1,0:T...) while((s32[]{:T(128)}, bf16[8,8,64,64]{3,2,1,0:T(8,128)(2,1)}, f32[8,8,64]{2,1,0:T(8,128)S(1)}, ...), condition=%wide.region_6.6_spmd, body=%wide.region_3.5_spmd.sunk | while | flops 136580608 | bytes 10903893 | solution.py:94
  1042.0 93.2 %while.99 = (s32[]{:T(128)}, bf16[8,8,64,64]{3,2,1,0:T(8,128)(2,1)}, f32[8,8,64]{2,1,0:T(8,128)S(1)}, bf16[8,8,64,64]{3,2,1,0:T(8,128)(2,1)}, s32[8,8,8]{2,1,0:T...) while((s32[]{:T(128)}, bf16[8,8,64,64]{3,2,1,0:T(8,128)(2,1)}, f32[8,8,64]{2,1,0:T(8,128)S(1)}, ...), condition=%wide.region_6.6_spmd, body=%wide.region_3.5_spmd.sunk | while | flops 136580608 | bytes 10903893 | solution.py:94
  1144.5 10.6 convolution_convert_fusion.5
  1155.1 99.4 %reduce-scatter.5.cloned.1.call-done = bf16[2048,1024]{1,0:T(8,128)(2,1)} async-done(((bf16[4096,1024]{1,0:T(8,128)(2,1)}), bf16[2048,1024]{1,0:T(8,128)(2,1)}) %reduce-scatter.5.cloned.1.call-update) | async-done | bytes 4194320 | tf_op jit(solution)/shard_map/reduce_scatter | solution.py:247
  1267.0 103.5 %all-gather.9.cloned.1.call-done = bf16[4096,1024]{1,0:T(8,128)(2,1)} async-done(((bf16[2048,1024]{1,0:T(8,128)(2,1)}), bf16[4096,1024]{1,0:T(8,128)(2,1)}) %all-gather.9.cloned.1.call-update) | async-done | bytes 8388624 | tf_op jit(solution)/shard_map/all_gather | solution.py:256
  1370.5 34.5 multiply_convert_fusion.2
  1405.0 70.9 %all-gather.11.cloned.1.call-done = bf16[4096,1024]{1,0:T(8,128)(2,1)} async-done(((bf16[2048,1024]{1,0:T(8,128)(2,1)}), bf16[4096,1024]{1,0:T(8,128)(2,1)}) %all-gather.11.cloned.1.call-update) | async-done | bytes 8388624 | tf_op jit(solution)/shard_map/all_gather | solution.py:257
  1475.9 45.3 fusion.101
  1521.1 23.7 convolution_convert_fusion.3
  1545.0 99.4 %reduce-scatter.9.cloned.1.call-done = bf16[2048,1024]{1,0:T(8,128)(2,1)} async-done(((bf16[4096,1024]{1,0:T(8,128)(2,1)}), bf16[2048,1024]{1,0:T(8,128)(2,1)}) %reduce-scatter.9.cloned.1.call-update) | async-done | bytes 4194320 | tf_op jit(solution)/shard_map/reduce_scatter | solution.py:276
  1644.4 8.9 fusion.86
  1653.9 7.1 fusion.94
  1661.1 24.3 convolution_convert_fusion.8
  1685.4 23.7 convolution_convert_fusion.7
  1709.2 56.0 %all-gather.13.cloned.1.call-done = bf16[4096,1024]{1,0:T(8,128)(2,1)} async-done(((bf16[2048,1024]{1,0:T(8,128)(2,1)}), bf16[4096,1024]{1,0:T(8,128)(2,1)}) %all-gather.13.cloned.1.call-update) | async-done | bytes 8388624 | tf_op jit(solution)/shard_map/all_gather | solution.py:286
  1765.2 10.1 convolution_convert_fusion.6
  1775.3 8.3 copy.97
  1783.7 10.2 convolution_convert_fusion.9
  1793.9 2905.6 %while.98 = (s32[]{:T(128)}, bf16[8,4096,64]{1,2,0:T(8,128)(2,1)}, bf16[8,4096,64]{1,2,0:T(8,128)(2,1)}, bf16[8,4096,64]{1,2,0:T(8,128)(2,1)}, bf16[8,4096,64]{2...) while((s32[]{:T(128)}, bf16[8,4096,64]{1,2,0:T(8,128)(2,1)}, ...), condition=%wide.region_22.23_spmd, body=%wide.region_17.22_spmd.sunk | while | flops 983490496 | bytes 111270584 | solution.py:298
  1817.9 307.3 %while.100 = (s32[]{:T(128)}, f32[64,8192]{1,0:T(8,128)}, f32[8,8,64,64]{3,2,1,0:T(8,128)}, s32[8,8,8]{2,1,0:T(8,128)S(1)}, bf16[8,8,64,64]{3,2,1,0:T(8,128)(2,1...) while((s32[]{:T(128)}, f32[64,8192]{1,0:T(8,128)}, ...), condition=%wide.region_20.20_spmd.clone, body=%wide.region_18.19_spmd.clone.sunk | while | flops 642031104 | bytes 48511176 | solution.py:174
  2181.8 306.4 %while.100 = (s32[]{:T(128)}, f32[64,8192]{1,0:T(8,128)}, f32[8,8,64,64]{3,2,1,0:T(8,128)}, s32[8,8,8]{2,1,0:T(8,128)S(1)}, bf16[8,8,64,64]{3,2,1,0:T(8,128)(2,1...) while((s32[]{:T(128)}, f32[64,8192]{1,0:T(8,128)}, ...), condition=%wide.region_20.20_spmd.clone, body=%wide.region_18.19_spmd.clone.sunk | while | flops 642031104 | bytes 48511176 | solution.py:174
  2544.7 306.4 %while.100 = (s32[]{:T(128)}, f32[64,8192]{1,0:T(8,128)}, f32[8,8,64,64]{3,2,1,0:T(8,128)}, s32[8,8,8]{2,1,0:T(8,128)S(1)}, bf16[8,8,64,64]{3,2,1,0:T(8,128)(2,1...) while((s32[]{:T(128)}, f32[64,8192]{1,0:T(8,128)}, ...), condition=%wide.region_20.20_spmd.clone, body=%wide.region_18.19_spmd.clone.sunk | while | flops 642031104 | bytes 48511176 | solution.py:174
  2907.7 306.4 %while.100 = (s32[]{:T(128)}, f32[64,8192]{1,0:T(8,128)}, f32[8,8,64,64]{3,2,1,0:T(8,128)}, s32[8,8,8]{2,1,0:T(8,128)S(1)}, bf16[8,8,64,64]{3,2,1,0:T(8,128)(2,1...) while((s32[]{:T(128)}, f32[64,8192]{1,0:T(8,128)}, ...), condition=%wide.region_20.20_spmd.clone, body=%wide.region_18.19_spmd.clone.sunk | while | flops 642031104 | bytes 48511176 | solution.py:174
  3270.6 306.4 %while.100 = (s32[]{:T(128)}, f32[64,8192]{1,0:T(8,128)}, f32[8,8,64,64]{3,2,1,0:T(8,128)}, s32[8,8,8]{2,1,0:T(8,128)S(1)}, bf16[8,8,64,64]{3,2,1,0:T(8,128)(2,1...) while((s32[]{:T(128)}, f32[64,8192]{1,0:T(8,128)}, ...), condition=%wide.region_20.20_spmd.clone, body=%wide.region_18.19_spmd.clone.sunk | while | flops 642031104 | bytes 48511176 | solution.py:174
  3633.6 306.4 %while.100 = (s32[]{:T(128)}, f32[64,8192]{1,0:T(8,128)}, f32[8,8,64,64]{3,2,1,0:T(8,128)}, s32[8,8,8]{2,1,0:T(8,128)S(1)}, bf16[8,8,64,64]{3,2,1,0:T(8,128)(2,1...) while((s32[]{:T(128)}, f32[64,8192]{1,0:T(8,128)}, ...), condition=%wide.region_20.20_spmd.clone, body=%wide.region_18.19_spmd.clone.sunk | while | flops 642031104 | bytes 48511176 | solution.py:174
  3996.5 306.4 %while.100 = (s32[]{:T(128)}, f32[64,8192]{1,0:T(8,128)}, f32[8,8,64,64]{3,2,1,0:T(8,128)}, s32[8,8,8]{2,1,0:T(8,128)S(1)}, bf16[8,8,64,64]{3,2,1,0:T(8,128)(2,1...) while((s32[]{:T(128)}, f32[64,8192]{1,0:T(8,128)}, ...), condition=%wide.region_20.20_spmd.clone, body=%wide.region_18.19_spmd.clone.sunk | while | flops 642031104 | bytes 48511176 | solution.py:174
  4359.5 306.4 %while.100 = (s32[]{:T(128)}, f32[64,8192]{1,0:T(8,128)}, f32[8,8,64,64]{3,2,1,0:T(8,128)}, s32[8,8,8]{2,1,0:T(8,128)S(1)}, bf16[8,8,64,64]{3,2,1,0:T(8,128)(2,1...) while((s32[]{:T(128)}, f32[64,8192]{1,0:T(8,128)}, ...), condition=%wide.region_20.20_spmd.clone, body=%wide.region_18.19_spmd.clone.sunk | while | flops 642031104 | bytes 48511176 | solution.py:174
  4710.7 17.6 bitcast_convert_fusion
  4728.3 23.4 convolution_convert_fusion.4
  4751.8 19.8 convert_bitcast_fusion.3
  4776.4 32.5 psum.69
  4809.4 6.9 convert_element_type.166
  4833.7 96.1 %reduce-scatter.7.cloned.1.call-done = bf16[2048,1024]{1,0:T(8,128)(2,1)} async-done(((bf16[4096,1024]{1,0:T(8,128)(2,1)}), bf16[2048,1024]{1,0:T(8,128)(2,1)}) %reduce-scatter.7.cloned.1.call-update) | async-done | bytes 4194320 | tf_op jit(solution)/shard_map/reduce_scatter | solution.py:261
  4929.8 17.7 fusion.80
  4947.5 43.1 all-reduce
  4990.7 188.7 %all-gather.15.cloned.1.call-done = bf16[48,1024,512]{2,1,0:T(8,128)(2,1)} async-done(((bf16[3,1024,512]{2,1,0:T(8,128)(2,1)}), bf16[48,1024,512]{2,1,0:T(8,128)(2,1)}) %all-gather.15.cloned.1.call-update) | async-done | bytes 50331664 | tf_op jit(solution)/shard_map/all_gather | solution.py:322
  5179.3 18.3 reduce_sum.195
  (2702 shorter events, 3928.0 us)
Async XLA Ops:
  7.2 116.7 %copy-start = (bf16[3,1024,512]{2,1,0:T(8,128)(2,1)S(1)}, bf16[3,1024,512]{2,1,0:T(8,128)(2,1)}, u32[]{:S(2)}) copy-start(bf16[3,1024,512]{2,1,0:T(8,128)(2,1)} %param.33) | copy-start | bytes 9437188
  7.2 6.8 copy-start.34
  7.2 6.8 copy-start.39
  7.2 116.7 %all-gather.7.cloned.1.call-start = ((), (), s32[]{:S(2)}) async-start(), calls=%async_computation.4 | async-start | bytes 12582912 | tf_op jit(solution)/shard_map/all_gather | solution.py:225
  7.3 6.7 copy-start.5
  10.3 7.1 copy-start.38
  17.0 1237.5 %reduce-scatter.5.cloned.1.call-start = ((), (), s32[]{:S(2)}) async-start(), calls=%async_computation.5 | async-start | bytes 12582912 | tf_op jit(solution)/shard_map/reduce_scatter | solution.py:247
  1144.4 10.6 copy-start.15
  1155.0 107.8 %copy-start.31 = (f32[1024]{0:T(1024)S(1)}, f32[1024]{0:T(1024)}, u32[]{:S(2)}) copy-start(f32[1024]{0:T(1024)} %param.35) | copy-start | bytes 12292
  1155.0 107.8 %copy-start.40 = (f32[1024]{0:T(1024)S(1)}, f32[1024]{0:T(1024)}, u32[]{:S(2)}) copy-start(f32[1024]{0:T(1024)} %param.36) | copy-start | bytes 12292
  1155.1 215.4 %all-gather.9.cloned.1.call-start = ((), (), s32[]{:S(2)}) async-start(), calls=%async_computation.6 | async-start | bytes 12582912 | tf_op jit(solution)/shard_map/all_gather | solution.py:256
  1254.5 4.8 copy-start.6
  1254.5 5.9 copy-start.10
  1262.9 107.6 %copy-start.43 = (f32[2048]{0:T(1024)S(1)}, f32[2048]{0:T(1024)}, u32[]{:S(2)}) copy-start(f32[2048]{0:T(1024)} %param.38) | copy-start | bytes 24580
  1266.3 209.5 %all-gather.11.cloned.1.call-start = ((), (), s32[]{:S(2)}) async-start(), calls=%async_computation.8 | async-start | bytes 12582912 | tf_op jit(solution)/shard_map/all_gather | solution.py:257
  1266.9 377.5 %reduce-scatter.9.cloned.1.call-start = ((), (), s32[]{:S(2)}) async-start(), calls=%async_computation.9 | async-start | bytes 12582912 | tf_op jit(solution)/shard_map/reduce_scatter | solution.py:276
  1544.9 99.5 %copy-start.18 = (f32[2048]{0:T(1024)S(1)}, f32[2048]{0:T(1024)}, u32[]{:S(2)}) copy-start(f32[2048]{0:T(1024)} %copy-done.17) | copy-start | bytes 24580
  1544.9 99.5 %copy-start.23 = (f32[2048]{0:T(1024)S(1)}, f32[2048]{0:T(1024)}, u32[]{:S(2)}) copy-start(f32[2048]{0:T(1024)} %copy-done.22) | copy-start | bytes 24580
  1544.9 99.5 %copy-start.32 = (f32[1024]{0:T(1024)S(1)}, f32[1024]{0:T(1024)}, u32[]{:S(2)}) copy-start(f32[1024]{0:T(1024)} %param.35) | copy-start | bytes 12292
  1544.9 220.3 %all-gather.13.cloned.1.call-start = ((), (), s32[]{:S(2)}) async-start(), calls=%async_computation.10 | async-start | bytes 12582912 | tf_op jit(solution)/shard_map/all_gather | solution.py:286
  1644.4 9.5 copy-start.7
  1644.4 9.5 copy-start.11
  1644.4 9.5 copy-start.12
  1661.1 3148.4 %all-reduce.4.cloned.1.call-start = ((), (), s32[]{:S(2)}) async-start(), calls=%async_computation.13 | async-start | bytes 18874368 | tf_op jit(solution)/shard_map/psum | solution.py:325
  1793.9 3033.7 %reduce-scatter.11.cloned.1.call-start = ((), (), s32[]{:S(2)}) async-start(), calls=%async_computation.11 | async-start | bytes 12582912 | tf_op jit(solution)/shard_map/reduce_scatter | solution.py:309
  1826.6 3.3 copy-start.2
  1903.1 3.3 copy-start.2
  2553.5 3.3 copy-start.2
  2629.6 3.3 copy-start.2
  3107.7 3.3 copy-start.2
  3680.0 3.3 copy-start.2
  4706.1 4.5 copy-start.13
  4728.3 201.5 %reduce-scatter.7.cloned.1.call-start = ((), (), s32[]{:S(2)}) async-start(), calls=%async_computation.7 | async-start | bytes 12582912 | tf_op jit(solution)/shard_map/reduce_scatter | solution.py:261
  4751.8 427.6 %all-gather.15.cloned.1.call-start = ((), (), s32[]{:S(2)}) async-start(), calls=%async_computation.12 | async-start | bytes 53477376 | tf_op jit(solution)/shard_map/all_gather | solution.py:322
  4771.6 4.7 copy-start.42
  4809.4 6.9 copy-start.14
  4816.3 4.5 copy-start.16
  4816.3 11.2 copy-start.21
  4816.3 11.2 copy-start.26
  4816.3 11.2 copy-start.35
  4820.8 109.0 %copy-start.19 = (f32[2048]{0:T(1024)S(1)}, f32[2048]{0:T(1024)}, u32[]{:S(2)}) copy-start(f32[2048]{0:T(1024)} %copy-done.17) | copy-start | bytes 24580
  4820.8 109.0 %copy-start.24 = (f32[2048]{0:T(1024)S(1)}, f32[2048]{0:T(1024)}, u32[]{:S(2)}) copy-start(f32[2048]{0:T(1024)} %copy-done.22) | copy-start | bytes 24580
  4820.8 109.0 %copy-start.28 = (f32[2048]{0:T(1024)S(1)}, f32[2048]{0:T(1024)}, u32[]{:S(2)}) copy-start(f32[2048]{0:T(1024)} %copy-done.27) | copy-start | bytes 24580
  4820.8 109.0 %copy-start.30 = (f32[2048]{0:T(1024)S(1)}, f32[2048]{0:T(1024)}, u32[]{:S(2)}) copy-start(f32[2048]{0:T(1024)} %copy-done.29) | copy-start | bytes 24580
  4820.8 109.0 %copy-start.33 = (f32[1024]{0:T(1024)S(1)}, f32[1024]{0:T(1024)}, u32[]{:S(2)}) copy-start(f32[1024]{0:T(1024)} %param.35) | copy-start | bytes 12292
  4820.8 109.0 %copy-start.41 = (f32[1024]{0:T(1024)S(1)}, f32[1024]{0:T(1024)}, u32[]{:S(2)}) copy-start(f32[1024]{0:T(1024)} %param.40) | copy-start | bytes 12292
  4833.7 113.9 %copy-start.36 = (f32[1024]{0:T(1024)S(1)}, f32[1024]{0:T(1024)}, u32[]{:S(2)}) copy-start(f32[1024]{0:T(1024)} %get-tuple-element.510) | copy-start | bytes 12292
  4833.7 113.9 %copy-start.37 = (f32[1024]{0:T(1024)S(1)}, f32[1024]{0:T(1024)}, u32[]{:S(2)}) copy-start(f32[1024]{0:T(1024)} %get-tuple-element.516) | copy-start | bytes 12292
  (216 other events, 336.2 us)
Sparse Core Ops, SparseCore 0:
  17.1 106.6 all-gather.6
  1155.2 99.3 reduce-scatter.4
  1266.5 103.9 all-gather.8
  1371.9 103.9 all-gather.10
  1545.0 99.3 reduce-scatter.8
  1661.2 103.9 all-gather.12
  1794.0 184.7 all-reduce.3
  4728.4 99.0 reduce-scatter.10
  4830.4 99.3 reduce-scatter.6
  4931.2 248.1 all-gather.14
